TPU v7x, 32 devices: a whole 2x2x4 slice. The times are simulated.
32 devices in a mesh: groups: 2 (over x), seq: 16 (over z, y, core).
Axes of the slice: x: 2, y: 2, z: 4, core: 2. Of those that a mesh axis runs over, the one named last changes fastest.
Arguments:
- query: bfloat16 [256, 4096], P(('groups', 'seq')), parts along dimension 0, may hold values from -4 to 4
- kv_pages: bfloat16 [1280, 2, 128, 512], P(('groups', 'seq')), parts along dimension 0, may hold values from -512 to 512
- page_table: int32 [256, 128], P('groups'), parts along dimension 0, may hold values from -1 to 639, as said below
- context_len: int32 [256], P('groups'), parts along dimension 0, may hold values from 1 to 16384, as said below
Outputs:
- attended: bfloat16 [256, 4096], P(('groups', 'seq')), parts along dimension 0
There are 2 independent parts, one for each index of `groups`. A program takes and returns all parts, laid end to end along the dimension named above; each array names one. Nothing has to cross between parts.
Inputs may be any that keep to these rules, and one draw needn't show every extreme that they name: `page_table`: entries of request r at slots below ceil(context_len[r] / 128) are page slots, no slot appears twice in the table; all other entries are -1. `context_len`: some request has exactly 16384 tokens.
All inputs are finite; a program needn't handle non-finite values.
Results may differ from a plain program's by a relative error of at most 0.0036.
Values may be sent and summed in bfloat16 or wider, within the bound.
A program may use at most 128 MiB of HBM per device.

v0:
```python
import jax
import jax.numpy as jnp
from jax import lax
from jax.sharding import PartitionSpec as P

HQ = 32
KVH = 4
DH = 128


def local(query, kv_pages, page_table, context_len):
    queries = lax.all_gather(query, "seq", axis=0, tiled=True)
    pages_dev = kv_pages.shape[0]
    page_len = kv_pages.shape[2]
    max_slots = page_table.shape[1]
    req_dev = query.shape[0]
    width = query.shape[1]
    groups = HQ // KVH
    scale = DH ** (-0.5)
    device = lax.axis_index("seq")
    global_page = device * pages_dev + jnp.arange(pages_dev, dtype=jnp.int32)
    matches = page_table[None, :, :] == global_page[:, None, None]
    owned = jnp.any(matches, axis=2)
    owner_hot = owned.astype(jnp.float32)
    slot_index = jnp.sum(
        jnp.where(matches, jnp.arange(max_slots, dtype=jnp.int32)[None, None, :], 0), axis=(1, 2)
    )
    page_length = jnp.sum(jnp.where(owned, context_len[None, :], 0), axis=1)
    positions = slot_index[:, None] * page_len + jnp.arange(page_len, dtype=jnp.int32)[None, :]
    valid = positions < page_length[:, None]
    page_query = jnp.dot(
        owned.astype(jnp.bfloat16), queries, preferred_element_type=jnp.float32
    ).astype(jnp.bfloat16)
    head_rows = page_query.reshape(pages_dev, KVH, groups, DH)
    keys = kv_pages[:, 0].reshape(pages_dev, page_len, KVH, DH)
    values = kv_pages[:, 1].reshape(pages_dev, page_len, KVH, DH)
    scores = (
        jnp.einsum("pgqd,ptgd->pgqt", head_rows, keys, preferred_element_type=jnp.float32) * scale
    )
    inside = valid[:, None, None, :]
    scores = jnp.where(inside, scores, jnp.float32(-1e30))
    page_peak = jnp.max(scores, axis=3).reshape(pages_dev, HQ)
    local_peak = jnp.max(
        jnp.where(owned[:, :, None], page_peak[:, None, :], jnp.float32(-1e30)), axis=0
    )
    global_peak = lax.pmax(local_peak, "seq")
    page_shift = jnp.dot(owner_hot, global_peak, precision=lax.Precision.HIGHEST).reshape(
        pages_dev, KVH, groups, 1
    )
    weights = jnp.where(inside, jnp.exp(scores - page_shift), jnp.float32(0.0))
    page_total = jnp.sum(weights, axis=3).reshape(pages_dev, HQ)
    page_numer = jnp.einsum(
        "pgqt,ptgd->pgqd", weights.astype(jnp.bfloat16), values, preferred_element_type=jnp.float32
    ).reshape(pages_dev, width)
    numer = jnp.dot(owner_hot.T, page_numer, precision=lax.Precision.HIGHEST)
    denom = jnp.dot(owner_hot.T, page_total, precision=lax.Precision.HIGHEST)
    mine_numer, mine_denom = (
        lax.psum_scatter(numer, "seq", scatter_dimension=0, tiled=True),
        lax.psum_scatter(denom, "seq", scatter_dimension=0, tiled=True),
    )
    result = mine_numer.reshape(req_dev, HQ, DH) / mine_denom.reshape(req_dev, HQ, 1)
    return result.reshape(req_dev, width).astype(jnp.bfloat16)


def solution(mesh):
    placed = (
        P(("groups", "seq"), None),
        P(("groups", "seq"), None, None, None),
        P("groups", None),
        P("groups"),
    )
    return jax.shard_map(
        local, mesh=mesh, in_specs=placed, out_specs=P(("groups", "seq"), None), check_vma=False
    )
```

profile of v0, /device:TPU:0, one launch (start us, length us, event | category | flops | bytes accessed | tf_op | source)
XLA Modules:
  0.0 191.9 jit_solution(4696091426273021620)
XLA Ops:
  6.5 0.0 all-gather.2.cloned.1.call-start
  6.5 0.7 all-gather.2.cloned.1.call-update
  7.3 0.0 reduce-scatter.2.cloned.1.call-start
  7.3 9.3 %fusion.20 = (bf16[40,1,128,512]{3,2,1,0:T(8,128)(2,1)}, bf16[40,1,128,512]{3,2,1,0:T(8,128)(2,1)}) fusion(bf16[40,2,128,512]{3,2,1,0:T(8,128)(2,1)} %param.5), kind=kLoop, calls=%fused_computation.31 | loop fusion | bytes 20971520 | tf_op jit(solution)/shard_map/slice | solution.py:35
  16.6 7.9 %copy.35 = bf16[40,1,128,512]{2,3,0,1:T(8,128)(2,1)} copy(bf16[40,1,128,512]{3,2,1,0:T(8,128)(2,1)} %get-tuple-element.6) | data formatting | bytes 10485760
  24.6 8.0 %copy.34 = bf16[40,1,128,512]{2,3,0,1:T(8,128)(2,1)} copy(bf16[40,1,128,512]{3,2,1,0:T(8,128)(2,1)} %get-tuple-element.5) | data formatting | bytes 10485760
  32.5 0.0 copy-done
  32.5 0.8 compare_reduce_fusion
  33.4 0.1 select_reduce_fusion.1
  33.5 0.9 fusion
  34.4 0.1 add_compare_fusion
  34.5 15.6 %all-gather.2.cloned.1.call-done = bf16[128,4096]{1,0:T(8,128)(2,1)} async-done(((bf16[8,4096]{1,0:T(8,128)(2,1)}), bf16[128,4096]{1,0:T(8,128)(2,1)}) %all-gather.2.cloned.1.call-update) | async-done | bytes 1048592 | tf_op jit(solution)/shard_map/all_gather | solution.py:12
  50.1 1.5 fusion.2
  51.6 0.1 copy.36
  51.6 3.5 %fusion.21 = (f32[40,4,8]{2,1,0:T(4,128)S(1)}, f32[40,4,8,128]{3,2,1,0:T(8,128)S(1)}) fusion(bf16[40,4,8,128]{3,2,1,0:T(8,128)(2,1)S(1)} %bitcast.36, bf16[40,128,4,128]{1,3,2,0:T(8,128)(2,1)} %bitcast.34, pred[40,128]{1,0:T(8,128)(4,1)S(1)} %add_compare_fusion), kind=kOutput, calls=%fused_computation.32 | convolution fusion | flops 42433280 | bytes 6236160 | tf_op jit(solution)/shard_map/pgqd,ptgd->pgqt/dot_general | solution.py:38
  55.2 0.1 copy.25
  55.2 0.1 copy.26
  55.3 0.2 select_reduce_fusion
  55.6 59.6 %pmax.7 = f32[4,8,128]{2,1,0:T(8,128)S(1)} all-reduce(f32[4,8,128]{2,1,0:T(8,128)S(1)} %bitcast.38), channel_id=1, replica_groups=mesh['groups'=2,'seq'=16] {'seq'}, use_global_device_ids=true, to_apply=%region_5.6 | all-reduce | flops 4096 | bytes 32768 | tf_op jit(solution)/shard_map/pmax | solution.py:46
  115.2 0.1 fusion.14
  115.3 0.1 copy.27
  115.5 0.0 copy-start.2
  115.5 4.8 %fusion.8 = f32[40,4,8,128]{3,2,1,0:T(8,128)S(1)} fusion(bf16[40,128,4,128]{1,3,2,0:T(8,128)(2,1)} %bitcast.33, f32[40,4,8,128]{3,2,1,0:T(8,128)S(1)} %get-tuple-element.8, f32[40,4,8]{2,1,0:T(4,128)S(1)} %copy.27, pred[40,128]{1,0:T(8,128)(4,1)S(1)} %add_compare_fusion), kind=kOutput, calls=%fused_computation.14 | convolution fusion | flops 42434560 | bytes 6563840 | tf_op jit(solution)/shard_map/pgqt,ptgd->pgqd/dot_general | solution.py:52
  120.2 2.7 %fusion.3 = f32[128,4096]{1,0:T(8,128)} fusion(pred[40,128]{1,0:T(8,128)(4,1)S(1)} %compare_reduce_fusion, f32[5,8,32,128]{3,2,1,0:T(8,128)S(1)} %bitcast.35), kind=kOutput, calls=%fused_computation.7 | convolution fusion | flops 251658240 | bytes 2757632 | tf_op jit(solution)/shard_map/dot_general | solution.py:55
  122.9 0.0 reduce-scatter.2.cloned.1.call-update
  123.0 0.6 dynamic-slice
  124.2 0.5 fusion.6
  124.7 0.1 copy.30
  124.8 0.3 fusion.16
  125.1 58.3 %all-reduce = f32[128,32]{1,0:T(8,128)S(1)} all-reduce(f32[128,32]{1,0:T(8,128)S(1)} %fusion.16), channel_id=3, replica_groups=mesh['groups'=2,'seq'=16] {'seq'}, use_global_device_ids=true, to_apply=%region_8.9.clone | all-reduce | flops 4096 | bytes 32768
  183.3 0.1 copy.31
  183.4 1.6 fusion.13
  (8 shorter events, 0.0 us)
Async XLA Ops:
  6.5 43.5 %all-gather.2.cloned.1.call-start = ((), (), s32[]{:S(2)}) async-start(), calls=%async_computation.1 | async-start | bytes 1114112 | tf_op jit(solution)/shard_map/all_gather | solution.py:12
  7.3 176.2 %reduce-scatter.2.cloned.1.call-start = ((), (), s32[]{:S(2)}) async-start(), calls=%async_computation.2 | async-start | bytes 2228224 | tf_op jit(solution)/shard_map/reduce_scatter | solution.py:58
  24.6 8.0 %copy-start = (s32[128,128]{1,0:T(8,128)S(1)}, s32[128,128]{1,0:T(8,128)}, u32[]{:S(2)}) copy-start(s32[128,128]{1,0:T(8,128)} %param.6) | copy-start | bytes 196612
  24.6 8.8 %copy-start.1 = (s32[128]{0:T(128)S(1)}, s32[128]{0:T(128)}, u32[]{:S(2)}) copy-start(s32[128]{0:T(128)} %param.7) | copy-start | bytes 1540
  115.5 7.5 %copy-start.2 = (u32[32]{0:T(128)S(1)}, u32[32]{0:T(128)}, u32[]{:S(2)}) copy-start(u32[32]{0:T(128)} %constant.24) | copy-start | bytes 388
Sparse Core Ops, SparseCore 0:
  9.5 40.5 all-gather.1
  123.1 59.1 reduce-scatter.1
where the time goes:
time: 192 us
  blocking collectives  118 us (61%)
  local copies, waits for them, and re-layouts  26.3 us (14%)
  waiting for transfers between devices  16.3 us (8%)
  between operations  14.1 us (7%)
  matrix products  12.8 us (7%)
  other arithmetic  4.37 us (2%)
    pmax x1, blocking collectives, local(): global_peak = lax.pmax(local_peak, 'seq')  59.6 us
    unnamed x1, blocking collectives  58.3 us
    unnamed x11, local copies, waits for them, and re-layouts  16.6 us
    all_gather x1, waiting for transfers between devices, local(): queries = lax.all_gather(query, 'seq', axis=0, tiled=True)  15.6 us
    slice x1, local copies, waits for them, and re-layouts, local(): keys = kv_pages[:, 0].reshape(pages_dev, page_len, KVH, DH)  9.32 us
    dot_general x1, matrix products, local(): jnp.einsum('pgqt,ptgd->pgqd', weights.astype(jnp.bfloat16), values, prefe...  4.75 us
  transfers between devices with their start and end apart: 2, of which 1 were waited for; matrix products, arithmetic and copies ran while one was open for 15% of the time, Pallas kernels for 0%

commit v1 on v0

v1 whole, which is shorter than its diff:
```python
import functools

import jax
import jax.numpy as jnp
from jax import lax
from jax.experimental import pallas as pl
from jax.experimental.pallas import tpu as pltpu
from jax.sharding import PartitionSpec as P

HQ = 32
KVH = 4
DH = 128
LOW = -1e30


def kernel(
    n, req_dev, pages_dev, page_len, scale,
    meta, q_ref, kv_ref, o_ref,
    kv, qg, qtmp, bd, pn, pm, pt, snd, rcv, mls, mlr, wts, wtt, acc,
    kv_sem, q_send, f_send, q_recv, a_send, a_recv, m_send, m_recv,
):
    me = lax.axis_index("seq")
    groups = HQ // KVH
    chips = n // 2
    sib = me + 1 - 2 * lax.rem(me, 2)
    per_block = 128 // req_dev
    blocks = n // per_block

    def kv_copy(p):
        return pltpu.make_async_copy(kv_ref.at[p], kv.at[p], kv_sem.at[p])

    @pl.loop(0, pages_dev)
    def _(p):
        kv_copy(p).start()

    barrier = pltpu.get_barrier_semaphore()

    @pl.loop(1, n)
    def _(k):
        pl.semaphore_signal(barrier, inc=1, device_id={"seq": lax.rem(me + k, n)})

    for h in range(HQ):
        qtmp[pl.ds(h, req_dev, stride=HQ), :] = q_ref[:, h * DH:(h + 1) * DH].astype(jnp.float32)
    qg[me] = qtmp[...].astype(jnp.bfloat16).reshape(req_dev, HQ, DH)
    row = lax.broadcasted_iota(jnp.int32, (HQ, KVH * DH), 0)
    col = lax.broadcasted_iota(jnp.int32, (HQ, KVH * DH), 1)
    bd[...] = jnp.where(row // groups == col // DH, 1.0, 0.0).astype(jnp.bfloat16)
    pn[pages_dev] = jnp.zeros((HQ, DH), jnp.float32)
    pt[pages_dev] = jnp.zeros((HQ, DH), jnp.float32)
    pm[pages_dev] = jnp.full((HQ, DH), LOW, jnp.float32)
    pl.semaphore_wait(barrier, n - 1)

    def q_copy(src, dst, sem):
        return pltpu.make_async_remote_copy(
            src_ref=qg.at[src], dst_ref=qg.at[src], send_sem=sem, recv_sem=q_recv.at[src],
            device_id={"seq": dst},
        )

    @pl.loop(1, chips)
    def _(k):
        q_copy(me, lax.rem(me + 2 * k, n), q_send.at[k]).start()

    q_copy(me, sib, f_send.at[0]).start()

    @pl.loop(1, chips)
    def _(k):
        src = lax.rem(me + n - 2 * k, n)
        q_copy(src, sib, q_send.at[k]).wait_recv()
        q_copy(src, sib, f_send.at[k]).start()

    @pl.loop(0, chips)
    def _(k):
        q_copy(lax.rem(sib + n - 2 * k, n), sib, f_send.at[k]).wait_recv()

    lane = lax.broadcasted_iota(jnp.int32, (HQ, page_len), 1)

    @pl.loop(0, pages_dev, unroll=4)
    def _(p):
        kv_copy(p).wait()
        q = qg[meta[p] // req_dev, lax.rem(meta[p], req_dev)]
        qb = jnp.concatenate([q] * KVH, axis=1) * bd[...]
        s = lax.dot_general(
            qb, kv[p, 0], (((1,), (1,)), ((), ())), preferred_element_type=jnp.float32
        ) * scale
        s = jnp.where(lane < meta[2 * pages_dev + p], s, LOW)
        m = jnp.max(s, axis=1, keepdims=True)
        e = jnp.exp(s - m)
        t = jnp.sum(e, axis=1, keepdims=True)
        full = jnp.dot(e.astype(jnp.bfloat16), kv[p, 1], preferred_element_type=jnp.float32)
        pn[p] = jnp.concatenate(
            [full[g * groups:(g + 1) * groups, g * DH:(g + 1) * DH] for g in range(KVH)], axis=0
        )
        pm[p] = jnp.broadcast_to(m, (HQ, DH))
        pt[p] = jnp.broadcast_to(t, (HQ, DH))

    @pl.loop(0, pages_dev)
    def _(p):
        b = meta[pages_dev + p]
        m0 = pm[b]
        m1 = pm[p]
        m = jnp.maximum(m0, m1)
        a0 = jnp.exp(m0 - m)
        a1 = jnp.exp(m1 - m)
        pn[p] = pn[b] * a0 + pn[p] * a1
        pt[p] = pt[b] * a0 + pt[p] * a1
        pm[p] = m

    wide = lax.broadcasted_iota(jnp.int32, (HQ, 128), 1)

    def ml_copy(d, k):
        return pltpu.make_async_remote_copy(
            src_ref=mls.at[d], dst_ref=mlr.at[me], send_sem=m_send.at[k], recv_sem=m_recv.at[me],
            device_id={"seq": d},
        )

    def ml_from(s):
        return pltpu.make_async_remote_copy(
            src_ref=mls.at[s], dst_ref=mlr.at[s], send_sem=m_send.at[0], recv_sem=m_recv.at[s],
            device_id={"seq": s},
        )

    def a_copy(d, k):
        return pltpu.make_async_remote_copy(
            src_ref=snd.at[d], dst_ref=rcv.at[me], send_sem=a_send.at[k], recv_sem=a_recv.at[me],
            device_id={"seq": d},
        )

    def a_from(s):
        return pltpu.make_async_remote_copy(
            src_ref=snd.at[s], dst_ref=rcv.at[s], send_sem=a_send.at[0], recv_sem=a_recv.at[s],
            device_id={"seq": s},
        )

    @pl.loop(0, blocks)
    def _(b):
        def put(c, carry):
            m, t = carry
            x = meta[3 * pages_dev + b * 128 + c]
            hit = wide == c
            return jnp.where(hit, pm[x], m), jnp.where(hit, pt[x], t)

        zero = jnp.zeros((HQ, 128), jnp.float32)
        m, t = lax.fori_loop(0, 128, put, (zero, zero), unroll=8)
        flip = jnp.concatenate([m, t, m, t], axis=0).T
        mls[pl.ds(b * per_block, per_block)] = flip.reshape(per_block, req_dev, 128)

    @pl.loop(1, n)
    def _(k):
        ml_copy(lax.rem(me + k, n), k).start()

    def fill(d):
        for i in range(req_dev):
            x = meta[3 * pages_dev + d * req_dev + i]
            t = pt[x]
            snd[d, i] = (pn[x] / jnp.where(t > 0, t, 1.0)).astype(jnp.bfloat16)

    @pl.loop(1, n)
    def _(k):
        d = lax.rem(me + k, n)
        fill(d)
        a_copy(d, k).start()

    fill(me)
    rcv[me] = snd[me]
    mlr[me] = mls[me]

    @pl.loop(1, n)
    def _(k):
        ml_from(lax.rem(me + n - k, n)).wait_recv()

    top = lax.fori_loop(0, n, lambda s, m: jnp.maximum(m, mlr[s]), mlr[0])

    def weigh(s, total):
        x = mlr[s]
        w = jnp.exp(x - top) * pltpu.roll(x, 128 - HQ, 1)
        wts[pl.ds(s * req_dev, req_dev), :] = w
        return total + w

    total = lax.fori_loop(0, n, weigh, jnp.zeros((req_dev, 128), jnp.float32))
    head = lax.broadcasted_iota(jnp.int32, (req_dev, 128), 1) < HQ
    inv = jnp.where(head, 1.0 / jnp.where(head, total, 1.0), 0.0)

    @pl.loop(0, n)
    def _(s):
        at = pl.ds(s * req_dev, req_dev)
        wts[at, :] = jnp.where(head, wts[at, :], 0.0) * inv

    @pl.loop(0, blocks)
    def _(b):
        wtt[b] = wts[pl.ds(b * 128, 128), :].T

    def add(s, first):
        w = wtt[s // per_block, 0:HQ, :]
        base = lax.rem(s, per_block) * req_dev
        for i in range(req_dev):
            c = jnp.sum(jnp.where(wide == base + i, w, 0.0), axis=1, keepdims=True)
            term = rcv[s, i].astype(jnp.float32) * c
            at = pl.ds(i * HQ, HQ)
            acc[at, :] = term if first else acc[at, :] + term

    add(me, True)

    @pl.loop(1, n)
    def _(k):
        s = lax.rem(me + n - k, n)
        a_from(s).wait_recv()
        add(s, False)

    for h in range(HQ):
        o_ref[:, h * DH:(h + 1) * DH] = acc[pl.ds(h, req_dev, stride=HQ), :].astype(jnp.bfloat16)

    @pl.loop(1, chips)
    def _(k):
        q_copy(me, sib, q_send.at[k]).wait_send()

    @pl.loop(0, chips)
    def _(k):
        q_copy(me, sib, f_send.at[k]).wait_send()

    @pl.loop(1, n)
    def _(k):
        d = lax.rem(me + k, n)
        ml_copy(d, k).wait_send()
        a_copy(d, k).wait_send()


def local(n, query, kv_pages, page_table, context_len):
    pages_dev = kv_pages.shape[0]
    page_len = kv_pages.shape[2]
    max_slots = page_table.shape[1]
    req_dev, width = query.shape
    reqs = page_table.shape[0]
    i32 = jnp.int32
    gp = lax.axis_index("seq") * pages_dev + jnp.arange(pages_dev, dtype=i32)
    none = reqs * max_slots
    spot = (
        jnp.arange(reqs, dtype=i32)[:, None] * max_slots + jnp.arange(max_slots, dtype=i32)[None, :]
    )
    code = jnp.min(
        jnp.where(page_table[None] == gp[:, None, None], spot[None], none), axis=(1, 2)
    )
    req = code // max_slots
    slot = code % max_slots
    ids = jnp.arange(pages_dev, dtype=i32)
    same = (req[:, None] == req[None, :]) & (ids[None, :] < ids[:, None]) & (code < none)[:, None]
    prev = jnp.max(jnp.where(same, ids[None, :], -1), axis=1)
    prev = jnp.where(prev < 0, pages_dev, prev)
    hot = req[:, None] == jnp.arange(reqs, dtype=i32)[None, :]
    length = jnp.sum(jnp.where(hot, context_len[None, :], 0), axis=1)
    vlen = jnp.where(code < none, jnp.clip(length - slot * page_len, 1, page_len), page_len)
    last = jnp.max(jnp.where(hot, ids[:, None], -1), axis=0)
    last = jnp.where(last < 0, pages_dev, last)
    meta = jnp.concatenate([jnp.where(code < none, req, 0), prev, vlen, last])
    f32, bf16 = jnp.float32, jnp.bfloat16
    dma = pltpu.SemaphoreType.DMA
    return pl.pallas_call(
        functools.partial(kernel, n, req_dev, pages_dev, page_len, DH ** (-0.5)),
        out_shape=jax.ShapeDtypeStruct((req_dev, width), bf16),
        in_specs=[
            pl.BlockSpec(memory_space=pltpu.SMEM),
            pl.BlockSpec(memory_space=pltpu.VMEM),
            pl.BlockSpec(memory_space=pl.ANY),
        ],
        out_specs=pl.BlockSpec(memory_space=pltpu.VMEM),
        scratch_shapes=[
            pltpu.VMEM(kv_pages.shape, bf16),
            pltpu.VMEM((n, req_dev, HQ, DH), bf16),
            pltpu.VMEM((req_dev * HQ, DH), f32),
            pltpu.VMEM((HQ, KVH * DH), bf16),
            pltpu.VMEM((pages_dev + 1, HQ, DH), f32),
            pltpu.VMEM((pages_dev + 1, HQ, DH), f32),
            pltpu.VMEM((pages_dev + 1, HQ, DH), f32),
            pltpu.VMEM((n, req_dev, HQ, DH), bf16),
            pltpu.VMEM((n, req_dev, HQ, DH), bf16),
            pltpu.VMEM((n, req_dev, 128), f32),
            pltpu.VMEM((n, req_dev, 128), f32),
            pltpu.VMEM((n * req_dev, 128), f32),
            pltpu.VMEM((n * req_dev // 128, 128, 128), f32),
            pltpu.VMEM((req_dev * HQ, DH), f32),
            dma((pages_dev,)),
            dma((n // 2,)),
            dma((n // 2,)),
            dma((n,)),
            dma((n,)),
            dma((n,)),
            dma((n,)),
            dma((n,)),
        ],
        compiler_params=pltpu.CompilerParams(
            collective_id=0, has_side_effects=True, vmem_limit_bytes=60 * 1024 * 1024
        ),
    )(meta, query, kv_pages)


def solution(mesh):
    placed = (
        P(("groups", "seq"), None),
        P(("groups", "seq"), None, None, None),
        P("groups", None),
        P("groups"),
    )
    return jax.shard_map(
        functools.partial(local, mesh.shape["seq"]),
        mesh=mesh, in_specs=placed, out_specs=P(("groups", "seq"), None), check_vma=False,
    )
```

time: 192 us -> 69.1 us (0.36)
  the two profiles are of different devices: /device:TPU:0 before, /device:TPU:29 now
where the time goes in v1:
time: 69.1 us; the launch traced here: 68.9 us
  Pallas kernels  63.8 us (92%)
  other arithmetic  3.57 us (5%)
  local copies, waits for them, and re-layouts  1.47 us (2%)
    pallas_call x1, Pallas kernels, local(): pl.pallas_call(functools.partial(kernel, n, req_dev, pages_dev, page_len,...  63.8 us
    reduce_min x1, other arithmetic, local(): jnp.min(jnp.where(page_table[None] == gp[:, None, None], spot[None], none...  1.77 us
    unnamed x1, local copies, waits for them, and re-layouts  1.47 us

profile of v1, /device:TPU:29, one launch (start us, length us, event | category | flops | bytes accessed | tf_op | source)
XLA Modules:
  0.0 68.9 jit_solution(10277514021733947167)
XLA Ops:
  0.0 0.1 iota_add_fusion
  0.1 1.8 %select_reduce_fusion = s32[40]{0:T(128)S(1)} fusion(s32[128,128]{1,0:T(8,128)S(1)} %iota_add_fusion, s32[128,128]{1,0:T(8,128)} %param.6, s32[40]{0:T(128)S(1)} %iota_add_fusion.1), kind=kLoop, calls=%fused_computation | loop fusion | flops 1966040 | bytes 131392 | tf_op jit(solution)/shard_map/reduce_min | solution.py:239
  1.9 0.2 select_reduce_fusion.3
  2.1 0.9 %select_reduce_fusion.2 = (s32[40]{0:T(128)S(1)}, s32[128]{0:T(128)S(1)}) fusion(s32[128]{0:T(128)} %param.7, s32[40]{0:T(128)S(1)} %get-tuple-element.8), kind=kLoop, calls=%fused_computation.3 | loop fusion | flops 25432 | bytes 1344 | tf_op jit(solution)/shard_map/reduce_sum | solution.py:249
  3.0 0.6 pad_add_fusion.meta
  3.6 63.8 %shard_map.46 = bf16[8,4096]{1,0:T(8,128)(2,1)} custom-call(s32[248]{0:T(256)} %pad_add_fusion.meta, bf16[8,4096]{1,0:T(8,128)(2,1)} %q_ref.1, bf16[40,2,128,512]{3,2,1,0:T(8,128)(2,1)} %kv_ref.1), custom_call_target="tpu_custom_call" | custom-call | tf_op jit(solution)/shard_map/pallas_call | solution.py:256
  67.4 1.5 %copy.6 = bf16[8,4096]{1,0:T(8,128)(2,1)} copy(bf16[8,4096]{1,0:T(8,128)(2,1)} %shard_map.46) | data formatting | bytes 131072
  (6 shorter events, 0.0 us)

commit v2 on v1

v2 whole, which is shorter than its diff:
```python
import functools

import jax
import jax.numpy as jnp
from jax import lax
from jax.experimental import pallas as pl
from jax.experimental.pallas import tpu as pltpu
from jax.sharding import PartitionSpec as P

HQ = 32
KVH = 4
DH = 128
LOW = -1e30


def kernel(
    n, req_dev, pages_dev, page_len, scale,
    table, ctx, q_ref, kv_ref, o_ref,
    kv, qg, qtmp, bd, pn, pm, pt, mv, meta, snd, rcx, mxs, mxr, cfs, out, rcv, mls, mlr, wts, wtt, acc,
    kv_sem, meta_sem, q_send, y_send, f_send, q_recv, x_send, x_recv, mx_send, mx_recv,
    a_send, a_recv, m_send, m_recv,
):
    me = lax.axis_index("seq")
    core = lax.rem(me, 2)
    chip = me // 2
    groups = HQ // KVH
    chips = n // 2
    rows = chips // 2
    zz = chip // 2
    yy = lax.rem(chip, 2)
    sib = chip * 2 + 1 - core
    per_block = 128 // req_dev
    blocks = n // per_block
    f32, i32, bf16 = jnp.float32, jnp.int32, jnp.bfloat16

    def dev(z, y):
        return (lax.rem(z + rows, rows) * 2 + y) * 2 + core

    ypeer = dev(zz, 1 - yy)

    def kv_copy(p):
        return pltpu.make_async_copy(kv_ref.at[p], kv.at[p], kv_sem.at[p])

    barrier = pltpu.get_barrier_semaphore()

    @pl.loop(1, n)
    def _(k):
        pl.semaphore_signal(barrier, inc=1, device_id={"seq": lax.rem(me + k, n)})

    @pl.loop(0, pages_dev)
    def _(p):
        kv_copy(p).start()

    for h in range(HQ):
        qtmp[pl.ds(h, req_dev, stride=HQ), :] = q_ref[:, h * DH:(h + 1) * DH].astype(f32)
    qg[me] = qtmp[...].astype(bf16).reshape(req_dev, HQ, DH)
    row = lax.broadcasted_iota(i32, (HQ, KVH * DH), 0)
    col = lax.broadcasted_iota(i32, (HQ, KVH * DH), 1)
    bd[...] = jnp.where(row // groups == col // DH, 1.0, 0.0).astype(bf16)
    pn[pages_dev] = jnp.zeros((HQ, DH), f32)
    pt[pages_dev] = jnp.zeros((HQ, DH), f32)
    pm[pages_dev] = jnp.full((HQ, DH), LOW, f32)
    wts[...] = jnp.zeros(wts.shape, f32)
    pl.semaphore_wait(barrier, n - 1)

    def q_copy(src, dst, sem):
        return pltpu.make_async_remote_copy(
            src_ref=qg.at[src], dst_ref=qg.at[src], send_sem=sem, recv_sem=q_recv.at[src],
            device_id={"seq": dst},
        )

    q_copy(me, ypeer, q_send.at[0]).start()

    @pl.loop(1, rows)
    def _(k):
        q_copy(me, dev(zz + k, yy), q_send.at[k]).start()

    q_copy(me, sib, f_send.at[0]).start()

    reqs, slots = table.shape
    none = reqs * slots
    lane1 = lax.broadcasted_iota(i32, (1, 128), 1)
    spot = lax.broadcasted_iota(i32, (reqs, slots), 0) * slots + lax.broadcasted_iota(
        i32, (reqs, slots), 1
    )

    def find(p, code):
        hit = jnp.where(table[...] == me * pages_dev + p, spot, none)
        best = jnp.min(jnp.min(hit, axis=0, keepdims=True), axis=1, keepdims=True)
        return jnp.where(lane1 == p, best, code)

    code = lax.fori_loop(0, pages_dev, find, jnp.full((1, 128), none, i32), unroll=4)
    req = code // slots
    sub = lax.broadcasted_iota(i32, (128, 128), 0)
    lanes = lax.broadcasted_iota(i32, (128, 128), 1)
    req_rows = jnp.broadcast_to(req, (128, 128))
    req_cols = req_rows.T
    live = code < none
    same = jnp.where((req_cols == req_rows) & (sub < lanes), sub, -1)
    prev = jnp.max(same, axis=0, keepdims=True)
    length = jnp.zeros((1, 128), i32)
    for b in range(reqs // 128):
        ctx_cols = jnp.broadcast_to(ctx[:, b * 128:(b + 1) * 128], (128, 128)).T
        length += jnp.sum(
            jnp.where(sub + b * 128 == req_rows, ctx_cols, 0), axis=0, keepdims=True
        )
        last = jnp.max(jnp.where(req_cols == lanes + b * 128, sub, -1), axis=0, keepdims=True)
        mv[3 + b:4 + b, :] = jnp.where(last < 0, pages_dev, last)
    mv[0:1, :] = jnp.where(live, req, 0)
    mv[1:2, :] = jnp.where(live & (prev >= 0), prev, pages_dev)
    left = jnp.minimum(jnp.maximum(length - (code - req * slots) * page_len, 1), page_len)
    mv[2:3, :] = jnp.where(live, left, page_len)
    meta_copy = pltpu.make_async_copy(mv, meta, meta_sem)
    meta_copy.start()

    @pl.loop(1, rows)
    def _(k):
        src = dev(zz - k, yy)
        q_copy(src, sib, f_send.at[k]).wait_recv()
        q_copy(src, ypeer, y_send.at[k]).start()
        q_copy(src, sib, f_send.at[k]).start()

    @pl.loop(0, rows)
    def _(k):
        src = dev(zz - k, 1 - yy)
        q_copy(src, sib, f_send.at[rows + k]).wait_recv()
        q_copy(src, sib, f_send.at[rows + k]).start()

    @pl.loop(0, pages_dev)
    def _(p):
        kv_copy(p).wait()

    meta_copy.wait()

    @pl.loop(0, chips)
    def _(k):
        q_copy(lax.rem(sib + n - 2 * k, n), sib, f_send.at[k]).wait_recv()

    lane = lax.broadcasted_iota(i32, (HQ, page_len), 1)
    batch = 8 if pages_dev % 8 == 0 else 1

    @pl.loop(0, pages_dev // batch)
    def _(c):
        ps = [c * batch + u for u in range(batch)]
        ss = []
        for p in ps:
            r = meta[0, p]
            q = qg[r // req_dev, lax.rem(r, req_dev)]
            qb = jnp.concatenate([q] * KVH, axis=1) * bd[...]
            s = lax.dot_general(
                qb, kv[p, 0], (((1,), (1,)), ((), ())), preferred_element_type=f32
            ) * scale
            ss.append(jnp.where(lane < meta[2, p], s, LOW))
        ms = [jnp.max(s, axis=1, keepdims=True) for s in ss]
        es = [jnp.exp(s - m) for s, m in zip(ss, ms)]
        ts = [jnp.sum(e, axis=1, keepdims=True) for e in es]
        ns = []
        for p, e in zip(ps, es):
            full = jnp.dot(e.astype(bf16), kv[p, 1], preferred_element_type=f32)
            ns.append(jnp.concatenate(
                [full[g * groups:(g + 1) * groups, g * DH:(g + 1) * DH] for g in range(KVH)],
                axis=0,
            ))
        for p, m, t, x in zip(ps, ms, ts, ns):
            pn[p] = x
            pm[p] = jnp.broadcast_to(m, (HQ, DH))
            pt[p] = jnp.broadcast_to(t, (HQ, DH))

    @pl.loop(0, pages_dev)
    def _(p):
        b = meta[1, p]
        m0 = pm[b]
        m1 = pm[p]
        m = jnp.maximum(m0, m1)
        a0 = jnp.exp(m0 - m)
        a1 = jnp.exp(m1 - m)
        pn[p] = pn[b] * a0 + pn[p] * a1
        pt[p] = pt[b] * a0 + pt[p] * a1
        pm[p] = m

    wide = lax.broadcasted_iota(i32, (HQ, 128), 1)

    def last_of(r):
        return meta[3 + r // 128, lax.rem(r, 128)]

    @pl.loop(0, blocks)
    def _(b):
        def put(c, carry):
            m, t = carry
            x = meta[3 + b, c]
            hit = wide == c
            return jnp.where(hit, pm[x], m), jnp.where(hit, pt[x], t)

        zero = jnp.zeros((HQ, 128), f32)
        m, t = lax.fori_loop(0, 128, put, (zero, zero), unroll=8)
        mxs[b, 0:HQ, :] = m
        mxs[b, HQ:2 * HQ, :] = t

    mx_copy = pltpu.make_async_remote_copy(
        src_ref=mxs, dst_ref=mxr, send_sem=mx_send, recv_sem=mx_recv, device_id={"seq": sib}
    )
    mx_copy.start()

    def x_copy(j):
        return pltpu.make_async_remote_copy(
            src_ref=snd.at[j], dst_ref=rcx.at[j], send_sem=x_send.at[j], recv_sem=x_recv.at[j],
            device_id={"seq": sib},
        )

    @pl.loop(1, chips + 1)
    def _(k):
        j = lax.rem(chip + k, chips)
        for i in range(req_dev):
            x = last_of((j * 2 + 1 - core) * req_dev + i)
            t = pt[x]
            snd[j, i] = (pn[x] / jnp.where(t > 0, t, 1.0)).astype(bf16)
        x_copy(j).start()

    mx_copy.wait_recv()

    @pl.loop(0, blocks)
    def _(b):
        m0, t0 = mxs[b, 0:HQ, :], mxs[b, HQ:2 * HQ, :]
        m1, t1 = mxr[b, 0:HQ, :], mxr[b, HQ:2 * HQ, :]
        m = jnp.maximum(m0, m1)
        e0 = jnp.exp(m0 - m)
        e1 = jnp.exp(m1 - m) * t1
        t = e0 * t0 + e1
        inv = 1.0 / jnp.where(t > 0, t, 1.0)
        cfs[b, 0:HQ, :] = e0 * inv
        cfs[b, HQ:2 * HQ, :] = e1 * inv
        flip = jnp.concatenate([m, t, m, t], axis=0).T
        mls[pl.ds(b * per_block, per_block)] = flip.reshape(per_block, req_dev, 128)

    def ml_copy(j):
        d = j * 2 + core
        return pltpu.make_async_remote_copy(
            src_ref=mls.at[d], dst_ref=mlr.at[chip], send_sem=m_send.at[j],
            recv_sem=m_recv.at[chip], device_id={"seq": d},
        )

    def ml_from(j):
        return pltpu.make_async_remote_copy(
            src_ref=mls.at[j], dst_ref=mlr.at[j], send_sem=m_send.at[j], recv_sem=m_recv.at[j],
            device_id={"seq": j * 2 + core},
        )

    def a_copy(j):
        return pltpu.make_async_remote_copy(
            src_ref=out.at[j], dst_ref=rcv.at[chip], send_sem=a_send.at[j],
            recv_sem=a_recv.at[chip], device_id={"seq": j * 2 + core},
        )

    def a_from(j):
        return pltpu.make_async_remote_copy(
            src_ref=out.at[j], dst_ref=rcv.at[j], send_sem=a_send.at[j], recv_sem=a_recv.at[j],
            device_id={"seq": j * 2 + core},
        )

    @pl.loop(1, chips)
    def _(k):
        ml_copy(lax.rem(chip + k, chips)).start()

    def merge(j, ref):
        x_copy(j).wait_recv()
        for i in range(req_dev):
            r = (j * 2 + core) * req_dev + i
            hit = jnp.concatenate([wide, wide], axis=0) == lax.rem(r, 128)
            c = jnp.sum(jnp.where(hit, cfs[r // 128], 0.0), axis=1, keepdims=True)
            mine = pn[last_of(r)] * c[0:HQ]
            ref[j, i] = (mine + rcx[j, i].astype(f32) * c[HQ:2 * HQ]).astype(bf16)

    @pl.loop(1, chips)
    def _(k):
        j = lax.rem(chip + k, chips)
        merge(j, out)
        a_copy(j).start()

    merge(chip, rcv)
    mlr[chip] = mls[me]

    @pl.loop(1, chips)
    def _(k):
        ml_from(lax.rem(chip + chips - k, chips)).wait_recv()

    top = lax.fori_loop(0, chips, lambda s, m: jnp.maximum(m, mlr[s]), mlr[0])

    def weigh(s, total):
        x = mlr[s]
        w = jnp.exp(x - top) * pltpu.roll(x, 128 - HQ, 1)
        wts[pl.ds(s * req_dev, req_dev), :] = w
        return total + w

    total = lax.fori_loop(0, chips, weigh, jnp.zeros((req_dev, 128), f32))
    head = lax.broadcasted_iota(i32, (req_dev, 128), 1) < HQ
    inv = jnp.where(head, 1.0 / jnp.where(head, total, 1.0), 0.0)

    @pl.loop(0, chips)
    def _(s):
        at = pl.ds(s * req_dev, req_dev)
        wts[at, :] = jnp.where(head, wts[at, :], 0.0) * inv

    @pl.loop(0, wts.shape[0] // 128)
    def _(b):
        wtt[b] = wts[pl.ds(b * 128, 128), :].T

    def add(s, first):
        w = wtt[s // per_block, 0:HQ, :]
        base = lax.rem(s, per_block) * req_dev
        for i in range(req_dev):
            c = jnp.sum(jnp.where(wide == base + i, w, 0.0), axis=1, keepdims=True)
            term = rcv[s, i].astype(f32) * c
            at = pl.ds(i * HQ, HQ)
            acc[at, :] = term if first else acc[at, :] + term

    add(chip, True)

    @pl.loop(1, chips)
    def _(k):
        s = lax.rem(chip + chips - k, chips)
        a_from(s).wait_recv()
        add(s, False)

    for h in range(HQ):
        o_ref[:, h * DH:(h + 1) * DH] = acc[pl.ds(h, req_dev, stride=HQ), :].astype(bf16)

    @pl.loop(0, rows)
    def _(k):
        q_copy(me, sib, q_send.at[k]).wait_send()

    @pl.loop(1, rows)
    def _(k):
        q_copy(me, sib, y_send.at[k]).wait_send()

    @pl.loop(0, chips)
    def _(k):
        q_copy(me, sib, f_send.at[k]).wait_send()
        x_copy(k).wait_send()

    mx_copy.wait_send()

    @pl.loop(1, chips)
    def _(k):
        j = lax.rem(chip + k, chips)
        ml_copy(j).wait_send()
        a_copy(j).wait_send()


def local(n, query, kv_pages, page_table, context_len):
    pages_dev, _, page_len, _ = kv_pages.shape
    req_dev, width = query.shape
    reqs = page_table.shape[0]
    blocks = reqs // 128
    chips = n // 2
    f32, bf16 = jnp.float32, jnp.bfloat16
    dma = pltpu.SemaphoreType.DMA
    vmem = pltpu.VMEM
    part = (chips, req_dev, HQ, DH)
    pages = (pages_dev + 1, HQ, DH)
    notes = ((3 + blocks + 7) // 8 * 8, 128)
    wide = (chips * req_dev + 127) // 128
    return pl.pallas_call(
        functools.partial(kernel, n, req_dev, pages_dev, page_len, DH ** (-0.5)),
        out_shape=jax.ShapeDtypeStruct((req_dev, width), bf16),
        in_specs=[
            pl.BlockSpec(memory_space=vmem),
            pl.BlockSpec(memory_space=vmem),
            pl.BlockSpec(memory_space=vmem),
            pl.BlockSpec(memory_space=pl.ANY),
        ],
        out_specs=pl.BlockSpec(memory_space=vmem),
        scratch_shapes=[
            vmem(kv_pages.shape, bf16),
            vmem((n, req_dev, HQ, DH), bf16),
            vmem((req_dev * HQ, DH), f32),
            vmem((HQ, KVH * DH), bf16),
            vmem(pages, f32),
            vmem(pages, f32),
            vmem(pages, f32),
            vmem(notes, jnp.int32),
            pltpu.SMEM(notes, jnp.int32),
            vmem(part, bf16),
            vmem(part, bf16),
            vmem((blocks, 2 * HQ, 128), f32),
            vmem((blocks, 2 * HQ, 128), f32),
            vmem((blocks, 2 * HQ, 128), f32),
            vmem(part, bf16),
            vmem(part, bf16),
            vmem((n, req_dev, 128), f32),
            vmem((chips, req_dev, 128), f32),
            vmem((wide * 128, 128), f32),
            vmem((wide, 128, 128), f32),
            vmem((req_dev * HQ, DH), f32),
            dma((pages_dev,)),
            dma,
            dma((chips // 2,)),
            dma((chips // 2,)),
            dma((chips,)),
            dma((n,)),
            dma((chips,)),
            dma((chips,)),
            dma,
            dma,
            dma((chips,)),
            dma((chips,)),
            dma((chips,)),
            dma((chips,)),
        ],
        compiler_params=pltpu.CompilerParams(
            collective_id=0, has_side_effects=True, vmem_limit_bytes=60 * 1024 * 1024
        ),
    )(page_table, context_len.reshape(1, reqs), query, kv_pages)


def solution(mesh):
    placed = (
        P(("groups", "seq"), None),
        P(("groups", "seq"), None, None, None),
        P("groups", None),
        P("groups"),
    )
    return jax.shard_map(
        functools.partial(local, mesh.shape["seq"]),
        mesh=mesh, in_specs=placed, out_specs=P(("groups", "seq"), None), check_vma=False,
    )
```

time: 69.1 us -> 39.3 us (0.57)
  the two profiles are of different devices: /device:TPU:29 before, /device:TPU:0 now
where the time goes in v2:
time: 39.3 us; the launch traced here: 38.7 us
  Pallas kernels  37.2 us (95%)
  local copies, waits for them, and re-layouts  1.47 us (4%)
    pallas_call x1, Pallas kernels, local(): pl.pallas_call(functools.partial(kernel, n, req_dev, pages_dev, page_len,...  37.2 us
    unnamed x1, local copies, waits for them, and re-layouts  1.47 us

profile of v2, /device:TPU:0, one launch (start us, length us, event | category | flops | bytes accessed | tf_op | source)
XLA Modules:
  0.0 38.7 jit_solution(6416106803070585119)
XLA Ops:
  0.0 37.2 %shard_map.46 = bf16[8,4096]{1,0:T(8,128)(2,1)} custom-call(s32[128,128]{1,0:T(8,128)} %table.1, s32[1,128]{1,0:T(1,128)} %bitcast.1, bf16[8,4096]{1,0:T(8,128)(2,1)} %q_ref.1, bf16[40,2,128,512]{3,2,1,0:T(8,128)(2,1)} %kv_ref.1), custom_call_target="tpu_custom_call" | custom-call | tf_op jit(solution)/shard_map/pallas_call | solution.py:362
  37.2 1.5 %copy.6 = bf16[8,4096]{1,0:T(8,128)(2,1)} copy(bf16[8,4096]{1,0:T(8,128)(2,1)} %shard_map.46) | data formatting | bytes 131072

commit v3 on v2

--- a/solution.py
+++ b/solution.py
@@ -43,9 +43,11 @@
 
     barrier = pltpu.get_barrier_semaphore()
 
-    @pl.loop(1, n)
-    def _(k):
-        pl.semaphore_signal(barrier, inc=1, device_id={"seq": lax.rem(me + k, n)})
+    pl.semaphore_signal(barrier, inc=1, device_id={"seq": sib})
+
+    @pl.loop(1, chips)
+    def _(k):
+        pl.semaphore_signal(barrier, inc=1, device_id={"seq": lax.rem(me + 2 * k, n)})
 
     @pl.loop(0, pages_dev)
     def _(p):
@@ -61,7 +63,7 @@
     pt[pages_dev] = jnp.zeros((HQ, DH), f32)
     pm[pages_dev] = jnp.full((HQ, DH), LOW, f32)
     wts[...] = jnp.zeros(wts.shape, f32)
-    pl.semaphore_wait(barrier, n - 1)
+    pl.semaphore_wait(barrier, chips)
 
     def q_copy(src, dst, sem):
         return pltpu.make_async_remote_copy(
@@ -137,7 +139,7 @@
         q_copy(lax.rem(sib + n - 2 * k, n), sib, f_send.at[k]).wait_recv()
 
     lane = lax.broadcasted_iota(i32, (HQ, page_len), 1)
-    batch = 8 if pages_dev % 8 == 0 else 1
+    batch = max(u for u in (20, 8, 4, 1) if pages_dev % u == 0)
 
     @pl.loop(0, pages_dev // batch)
     def _(c):

time: 39.3 us -> 38 us (0.967)
  Pallas kernels: 37.2 us -> 35.9 us
    pallas_call x1, Pallas kernels: 37.2 us -> 35.9 us  [local(): pl.pallas_call(functools.partial(kernel, n, req_dev, pages_dev, page_len,...]
where the time goes in v3:
time: 38 us; the launch traced here: 37.4 us
  Pallas kernels  35.9 us (94%)
  local copies, waits for them, and re-layouts  1.47 us (4%)
    pallas_call x1, Pallas kernels, local(): pl.pallas_call(functools.partial(kernel, n, req_dev, pages_dev, page_len,...  35.9 us
    unnamed x1, local copies, waits for them, and re-layouts  1.47 us

profile of v3, /device:TPU:0, one launch (start us, length us, event | category | flops | bytes accessed | tf_op | source)
XLA Modules:
  0.0 37.4 jit_solution(3125193698990600701)
XLA Ops:
  0.0 35.9 %shard_map.46 = bf16[8,4096]{1,0:T(8,128)(2,1)} custom-call(s32[128,128]{1,0:T(8,128)} %table.1, s32[1,128]{1,0:T(1,128)} %bitcast.1, bf16[8,4096]{1,0:T(8,128)(2,1)} %q_ref.1, bf16[40,2,128,512]{3,2,1,0:T(8,128)(2,1)} %kv_ref.1), custom_call_target="tpu_custom_call" | custom-call | tf_op jit(solution)/shard_map/pallas_call | solution.py:364
  35.9 1.5 %copy.6 = bf16[8,4096]{1,0:T(8,128)(2,1)} copy(bf16[8,4096]{1,0:T(8,128)(2,1)} %shard_map.46) | data formatting | bytes 131072
